TPU v7x, 32 devices: a whole 2x2x4 slice. The times are simulated.
32 devices in a mesh: xy: 2 (over core), gz: 4 (over y, x), ta: 4 (over z).
Axes of the slice: x: 2, y: 2, z: 4, core: 2. Of those that a mesh axis runs over, the one named last changes fastest.
Arguments:
- right_side: float32 [2, 4, 4, 128, 128], P('xy', 'gz', 'ta'), may hold values from -40 to 40
- link_blocks: float32 [2, 4, 4, 9, 2, 32, 32, 128], P('xy', 'gz', 'ta'), may hold values from -0.75 to 0.75
Outputs:
- solution: float32 [2, 4, 4, 128, 128], P('xy', 'gz', 'ta')
- residual: float32 [2, 4, 4, 128, 128], P('xy', 'gz', 'ta')
All inputs are finite; a program needn't handle non-finite values.
Results may differ from a plain program's by a relative error of at most 0.00018.
Values sent between devices are 32-bit elements; how exact they have to be, the bound alone decides.
A program may use at most 128 MiB of HBM per device.

v0:
```python
import functools

import jax
import jax.numpy as jnp
from jax import lax
from jax.experimental import pallas as pl
from jax.experimental.pallas import tpu as pltpu
from jax.sharding import PartitionSpec as P

DOF = 32
RHS = 2
NY = 8
CZ = 2
CT = 8
S = 128
E = 128
MESH = pl.DeviceIdType.MESH

mass_shift = 4.0
epsilon = 1e-06


def cmul(a, b):
    return (a[0] * b[0] - a[1] * b[1], a[0] * b[1] + a[1] * b[0])


def conj(a):
    return (a[0], -a[1])


def cadd(a, b):
    return (a[0] + b[0], a[1] + b[1])


def csub(a, b):
    return (a[0] - b[0], a[1] - b[1])


def scale(a, x):
    return (a[0] * x, a[1] * x)


def size2(a):
    return a[0] * a[0] + a[1] * a[1]


def coefficients(g00, g11, g22, g01, g02, g12):
    beta2 = g00 + epsilon
    beta = jnp.sqrt(beta2)
    inv_beta2 = 1.0 / beta2
    h00 = scale((mass_shift * g00 + g01[0], g01[1]), inv_beta2)
    a = (mass_shift - h00[0], -h00[1])
    left = g11 + size2(a) * g00 + 2.0 * cmul(conj(a), g01)[0]
    h10_2 = jnp.maximum(left, 0.0) * inv_beta2 + epsilon
    h10 = jnp.sqrt(h10_2)
    a4 = (a[0] + mass_shift, a[1])
    a_4 = scale(a, mass_shift)
    top = cadd(cadd(g02, cmul(a4, g01)), scale(a_4, g00))
    h01 = scale(top, inv_beta2 / h10)
    low = cadd(cadd(g12, scale(a4, g11)), cmul(a_4, conj(g01)))
    h11 = scale(cadd(low, cmul(conj(a), top)), inv_beta2 / h10_2)
    p = csub(a4, h11)
    q = csub(csub(a_4, scale(h01, h10)), cmul(h11, a))
    left = g22 + size2(p) * g11 + size2(q) * g00
    left = left + 2.0 * (
        cmul(p, conj(g12))[0] + cmul(q, conj(g02))[0] + cmul(cmul(conj(q), p), g01)[0]
    )
    h21_2 = jnp.maximum(left, 0.0) * (inv_beta2 / h10_2) + epsilon
    m00 = size2(h00) + h10_2
    m01 = cadd(cmul(conj(h00), h01), scale(h11, h10))
    m11 = size2(h01) + size2(h11) + h21_2
    t0 = scale(conj(h00), beta)
    t1 = scale(conj(h01), beta)
    inv_l0 = 1.0 / jnp.sqrt(m00)
    l10 = scale(conj(m01), inv_l0)
    f0 = scale(t0, inv_l0)
    inv_d = 1.0 / (m11 - size2(l10))
    y1 = scale(csub(t1, cmul(l10, f0)), inv_d)
    y0 = scale(csub(f0, cmul(conj(l10), y1)), inv_l0)
    inv_beta = 1.0 / beta
    wb = scale(y1, inv_beta / h10)
    wa = cadd(scale(y0, inv_beta), cmul(wb, a))
    return wa, wb


def kernel(
    sizes, b_hbm, l_hbm, sol_ref, res_ref,
    links, field, xbuf, zbuf, tface, tbuf, turned, acc, red,
    b_sem, l_sem, send_sem, recv_sem, sum_send, sum_recv,
):
    nx, nz, nt = sizes
    total_count = nx * nz * nt
    ix, iz, it = lax.axis_index("xy"), lax.axis_index("gz"), lax.axis_index("ta")
    here = (ix * nz + iz) * nt + it

    def step(axis_value, by, count):
        return lax.rem(axis_value + (by + count), count)

    def mate(delta):
        other = lax.rem(here + delta, total_count)
        plane = other // nt
        return (plane // nz, lax.rem(plane, nz), lax.rem(other, nt))

    order = [0, 3, 4, 1, 2, 7, 8, 5, 6]
    b_copy = pltpu.make_async_copy(b_hbm.at[0, 0, 0], field.at[0], b_sem)
    b_copy.start()
    l_copies = {}
    for k in order:
        l_copies[k] = pltpu.make_async_copy(l_hbm.at[0, 0, 0, k], links.at[k], l_sem.at[k])
        l_copies[k].start()

    barrier = pltpu.get_barrier_semaphore()
    for delta in range(1, total_count):
        pl.semaphore_signal(barrier, inc=1, device_id=mate(delta), device_id_type=MESH)
    pl.semaphore_wait(barrier, total_count - 1)
    b_copy.wait()

    lane = lax.broadcasted_iota(jnp.int32, (S, E), 1)
    in_t = lane % CT
    in_z = (lane // CT) % CZ
    row8 = lax.broadcasted_iota(jnp.int32, (8, 128), 0)

    def halo(n):
        mine = field.at[n]
        tface[n, 0] = field[n, pl.ds(0, NY * CZ, stride=CT), :]
        tface[n, 1] = field[n, pl.ds(CT - 1, NY * CZ, stride=CT), :]
        tiles = mine.reshape(NY, CZ, CT, E)
        moves = []
        for way in (0, 1):
            by = 1 if way else -1
            moves.append(("t%d" % way, tface.at[n, way], tbuf.at[n, way], (ix, iz, step(it, by, nt))))
        for way in (0, 1):
            by = 1 if way else -1
            moves.append(
                ("z%d" % way, tiles.at[:, way * (CZ - 1)], zbuf.at[n].reshape(NY, CZ, CT, E).at[:, (1 - way) * (CZ - 1)],
                 (ix, step(iz, by, nz), it))
            )
        for way in (0, 1) if nx > 2 else (0,):
            by = 1 if way else -1
            moves.append(("x%d" % way, mine, xbuf.at[n, way], (step(ix, by, nx), iz, it)))
        copies = {}
        for number, (name, source, target, device) in enumerate(moves):
            copy = pltpu.make_async_remote_copy(
                src_ref=source, dst_ref=target,
                send_sem=send_sem.at[n, number], recv_sem=recv_sem.at[n, number],
                device_id=device, device_id_type=MESH,
            )
            copy.start()
            copies[name] = copy
        return copies

    def products(passes, fresh, merge=False):
        def body(c, carry):
            if fresh:
                sums = [jnp.zeros((8, 128), jnp.float32) for _ in range(4)]
            else:
                sums = [acc[i, c] for i in range(4)]
            for link, near in passes:
                for j in range(DOF // 8):
                    rows = pl.ds(8 * j, 8)
                    lr = links[link, 0, c, rows, :]
                    li = links[link, 1, c, rows, :]
                    if merge:
                        lr = lr + links[link + 1, 0, c, rows, :]
                        li = li + links[link + 1, 1, c, rows, :]
                        links[link, 0, c, rows, :] = lr
                        links[link, 1, c, rows, :] = li
                    for r in range(RHS):
                        vr = turned[near, pl.ds(2 * r * DOF + 8 * j, 8), :]
                        vi = turned[near, pl.ds((2 * r + 1) * DOF + 8 * j, 8), :]
                        sums[2 * r] = sums[2 * r] + lr * vr - li * vi
                        sums[2 * r + 1] = sums[2 * r + 1] + lr * vi + li * vr
            for i in range(4):
                acc[i, c] = sums[i]
            return carry

        lax.fori_loop(0, DOF, body, 0, unroll=2)

    lane8 = lax.broadcasted_iota(jnp.int32, (8, 128), 1)

    def split_links():
        inner = (lane8 // CT) % CZ == 0
        last = lane8 % CT == CT - 1

        def body(c, carry):
            for p in range(2):
                for j in range(DOF // 8):
                    rows = pl.ds(8 * j, 8)
                    up, down = links[5, p, c, rows, :], links[6, p, c, rows, :]
                    links[5, p, c, rows, :] = jnp.where(inner, up, down)
                    links[6, p, c, rows, :] = jnp.where(inner, down, up)
                    up, down = links[7, p, c, rows, :], links[8, p, c, rows, :]
                    links[9, p, c, rows, :] = jnp.where(last, up, down)
            return carry

        lax.fori_loop(0, DOF, body, 0, unroll=2)

    def fold(xs):
        low = row8 < 4
        ys = [
            jnp.where(low, xs[i], xs[i + 4]) + pltpu.roll(jnp.where(low, xs[i + 4], xs[i]), 4, 0)
            for i in range(4)
        ]
        low = row8 % 4 < 2
        zs = [
            jnp.where(low, ys[i] + pltpu.roll(ys[i], 6, 0), ys[i + 2] + pltpu.roll(ys[i + 2], 2, 0))
            for i in range(2)
        ]
        return jnp.where(
            row8 % 2 < 1, zs[0] + pltpu.roll(zs[0], 7, 0), zs[1] + pltpu.roll(zs[1], 1, 0)
        )

    def apply(n, copies):
        own = turned[0]
        turned[3] = pltpu.roll(own, S - CZ * CT, 1)
        turned[4] = pltpu.roll(own, CZ * CT, 1)
        turned[5] = jnp.where(in_z == 0, pltpu.roll(own, S - CT, 1), pltpu.roll(own, CT, 1))
        turned[7] = jnp.where(in_t == CT - 1, 0.0, pltpu.roll(own, S - 1, 1))
        turned[8] = jnp.where(in_t == 0, 0.0, pltpu.roll(own, 1, 1))
        if n == 0:
            for k in range(9):
                l_copies[k].wait()
            split_links()
        products(((0, 0), (3, 3), (4, 4)), True)
        products(((5, 5), (7, 7), (8, 8)), False)
        copies["x0"].wait_recv()
        turned[1] = xbuf[n, 0].T
        if nx > 2:
            copies["x1"].wait_recv()
            turned[2] = xbuf[n, 1].T
            products(((1, 1), (2, 2)), False)
        else:
            products(((1, 1),), False, n == 0)
        copies["z0"].wait_recv()
        copies["z1"].wait_recv()
        turned[6] = zbuf[n].T
        products(((6, 6),), False)
        copies["t0"].wait_recv()
        copies["t1"].wait_recv()
        edge = field.at[3]
        edge[pl.ds(CT - 1, NY * CZ, stride=CT), :] = tbuf[n, 0]
        edge[pl.ds(0, NY * CZ, stride=CT), :] = tbuf[n, 1]
        turned[9] = edge[...].T
        products(((9, 9),), False)
        for i in range(4):
            for c in range(0, DOF, 8):
                turned[0, pl.ds(i * DOF + c, 8), :] = fold([acc[i, c + j] for j in range(8)])
        field[n + 1] = turned[0].T

    field[3] = jnp.zeros((S, E), jnp.float32)
    first = halo(0)
    turned[0] = field[0].T
    apply(0, first)
    second = halo(1)
    apply(1, second)

    in_p = (lax.broadcasted_iota(jnp.int32, (S, E), 1) // DOF) % 2

    def aside(v):
        return jnp.where(in_p == 0, pltpu.roll(v, E - DOF, 1), -pltpu.roll(v, DOF, 1))

    def total(u, v):
        return jnp.sum((u * v).reshape(S // 8, 8, E), axis=0)

    k0, k1, k2 = field[0], field[1], field[2]
    z1, z2 = aside(k1), aside(k2)
    sums = [
        total(k0, k0), total(k1, k1), total(k2, k2), total(k0, k1), total(k0, z1),
        total(k0, k2), total(k0, z2),
    ]
    first_p = in_p[:8] == 0

    def both(v):
        return v + jnp.where(first_p, pltpu.roll(v, E - DOF, 1), pltpu.roll(v, DOF, 1))

    sums.append(jnp.where(first_p, both(total(k1, k2)), both(total(k1, z2))))
    lanes = fold(sums)
    for width in (16, 8, 4):
        low = lane8 % (2 * width) < width
        lanes = lanes + jnp.where(
            low, pltpu.roll(lanes, 128 - width, 1), pltpu.roll(lanes, width, 1)
        )
    seat = (lane8 % DOF) // 4 == row8
    red[0] = jnp.sum(jnp.where(seat, lanes, 0.0), axis=0, keepdims=True)
    sent = []
    for delta in range(1, total_count):
        copy = pltpu.make_async_remote_copy(
            src_ref=red.at[0], dst_ref=red.at[delta],
            send_sem=sum_send.at[delta], recv_sem=sum_recv.at[delta],
            device_id=mate(delta), device_id_type=MESH,
        )
        copy.start()
        sent.append(copy)
    for copy in sent:
        copy.wait_recv()
    value = jnp.where(seat, jnp.sum(red[...], axis=0), 0.0)
    quarter = lax.broadcasted_iota(jnp.int32, (8, 128), 1) // DOF
    sum00, sum01, sum10, sum11 = [
        jnp.sum(jnp.where(quarter == i, value, 0.0), axis=1, keepdims=True) for i in range(4)
    ]
    half = quarter < 2
    gram = jnp.where(half, sum00 + sum01, sum10 + sum11)
    g = [gram[i : i + 1] for i in range(7)]
    g.append(jnp.where(half, sum00, sum10)[7:8])
    g.append(jnp.where(half, sum01, sum11)[7:8])
    wa, wb = coefficients(g[0], g[1], g[2], (g[3], g[4]), (g[5], g[6]), (g[7], g[8]))

    def weighted(w, v, z):
        return w[0] * v - w[1] * z

    k0, k1, k2 = field[0], field[1], field[2]
    z0, z1, z2 = aside(k0), aside(k1), aside(k2)
    sol = weighted(wa, k0, z0) + weighted(wb, k1, z1)
    image = weighted(wa, k1, z1) + weighted(wb, k2, z2)
    sol_ref[0, 0, 0] = sol
    res_ref[0, 0, 0] = k0 - mass_shift * sol - image
    for copies in (first, second):
        for copy in copies.values():
            copy.wait_send()
    for copy in sent:
        copy.wait_send()


def deliver(a_ref, b_ref, sol_ref, res_ref):
    sol_ref[...] = a_ref[...]
    res_ref[...] = b_ref[...]


def shards(sizes, right_side, link_blocks):
    nx, nz, nt = sizes
    out = jax.ShapeDtypeStruct(right_side.shape, jnp.float32)
    f32 = jnp.float32
    moves = 6 if nx > 2 else 5
    held = pltpu.VMEM(right_side.shape, f32)
    results = pl.pallas_call(
        functools.partial(kernel, sizes),
        out_shape=(held, held),
        in_specs=[pl.BlockSpec(memory_space=pl.ANY)] * 2,
        out_specs=(pl.BlockSpec(memory_space=pltpu.VMEM),) * 2,
        scratch_shapes=[
            pltpu.VMEM((10, 2, DOF, DOF, S), f32),
            pltpu.VMEM((4, S, E), f32),
            pltpu.VMEM((2, 2, S, E), f32),
            pltpu.VMEM((2, S, E), f32),
            pltpu.VMEM((2, 2, NY * CZ, E), f32),
            pltpu.VMEM((2, 2, NY * CZ, E), f32),
            pltpu.VMEM((10, E, S), f32),
            pltpu.VMEM((4, DOF, 8, S), f32),
            pltpu.VMEM((nx * nz * nt, 1, 128), f32),
            pltpu.SemaphoreType.DMA,
            pltpu.SemaphoreType.DMA((9,)),
            pltpu.SemaphoreType.DMA((2, moves)),
            pltpu.SemaphoreType.DMA((2, moves)),
            pltpu.SemaphoreType.DMA((nx * nz * nt,)),
            pltpu.SemaphoreType.DMA((nx * nz * nt,)),
        ],
        compiler_params=pltpu.CompilerParams(
            collective_id=0, has_side_effects=True, vmem_limit_bytes=56 * 1024 * 1024
        ),
    )(right_side, link_blocks)
    return pl.pallas_call(
        deliver,
        out_shape=(out, out),
        in_specs=[pl.BlockSpec(memory_space=pltpu.VMEM)] * 2,
        out_specs=(pl.BlockSpec(memory_space=pltpu.VMEM),) * 2,
    )(*[pltpu.with_memory_space_constraint(x, pltpu.VMEM) for x in results])


def solution(mesh):
    sizes = tuple(mesh.shape[name] for name in ("xy", "gz", "ta"))
    return jax.shard_map(
        functools.partial(shards, sizes),
        mesh=mesh,
        in_specs=(
            P("xy", "gz", "ta", None, None),
            P("xy", "gz", "ta", None, None, None, None, None),
        ),
        out_specs=(P("xy", "gz", "ta", None, None), P("xy", "gz", "ta", None, None)),
        check_vma=False,
    )
```

profile of v0, /device:TPU:0, one launch (start us, length us, event | category | flops | bytes accessed | tf_op | source)
XLA Modules:
  0.0 24.1 jit_solution(17189979057661250419)
XLA Ops:
  0.6 22.8 %shard_map.41 = (f32[1,1,1,128,128]{4,3,2,1,0:T(8,128)S(1)}, f32[1,1,1,128,128]{4,3,2,1,0:T(8,128)S(1)}) custom-call(f32[1,1,1,128,128]{4,3,2,1,0:T(8,128)} %b_hbm.1, f32[1,1,1,9,2,32,32,128]{7,6,5,4,3,2,1,0:T(8,128)} %l_hbm.1), custom_call_target="tpu_custom_call" | custom-call | tf_op jit(solution)/shard_map/pallas_call | solution.py:335
  23.4 0.7 %shard_map.42 = (f32[1,1,1,128,128]{4,3,2,1,0:T(8,128)}, f32[1,1,1,128,128]{4,3,2,1,0:T(8,128)}) custom-call(f32[1,1,1,128,128]{4,3,2,1,0:T(8,128)S(1)} %get-tuple-element.4.a_ref, f32[1,1,1,128,128]{4,3,2,1,0:T(8,128)S(1)} %get-tuple-element.5.b_ref), custom_call_target="tpu_custom_call" | custom-call | tf_op jit(solution)/shard_map/pallas_call | solution.py:361
where the time goes:
time: 24.2 us; the launch traced here: 24.1 us
  Pallas kernels  23.4 us (97%)
  between operations  0.64 us (3%)
    pallas_call x1, Pallas kernels, shards(): pl.pallas_call(functools.partial(kernel, sizes), out_shape=(held, held),...  22.8 us
    pallas_call x1, Pallas kernels, shards(): pl.pallas_call(deliver, out_shape=(out, out), in_specs=[pl.BlockSpec(memo...  0.66 us

commit v1 on v0

--- a/solution.py
+++ b/solution.py
@@ -86,7 +86,7 @@
 def kernel(
     sizes, b_hbm, l_hbm, sol_ref, res_ref,
     links, field, xbuf, zbuf, tface, tbuf, turned, acc, red,
-    b_sem, l_sem, send_sem, recv_sem, sum_send, sum_recv,
+    b_sem, l_sem, send_sem, recv_sem, sum_send, sum_recv, seen_z, seen_x,
 ):
     nx, nz, nt = sizes
     total_count = nx * nz * nt
@@ -109,10 +109,18 @@
         l_copies[k] = pltpu.make_async_copy(l_hbm.at[0, 0, 0, k], links.at[k], l_sem.at[k])
         l_copies[k].start()
 
+    line_x = [(step(ix, d, nx), iz, it) for d in range(1, nx)]
+    line_z = [(ix, step(iz, d, nz), it) for d in range(1, nz)]
+    line_t = [(ix, iz, step(it, d, nt)) for d in range(1, nt)]
+
+    def tell(sem, devices):
+        for device in devices:
+            pl.semaphore_signal(sem, inc=1, device_id=device, device_id_type=MESH)
+
     barrier = pltpu.get_barrier_semaphore()
-    for delta in range(1, total_count):
-        pl.semaphore_signal(barrier, inc=1, device_id=mate(delta), device_id_type=MESH)
-    pl.semaphore_wait(barrier, total_count - 1)
+    tell(barrier, line_t + line_z + line_x)
+    pl.semaphore_wait(barrier, len(line_t) + len(line_z) + len(line_x))
+    tell(seen_z, line_z)
     b_copy.wait()
 
     lane = lax.broadcasted_iota(jnp.int32, (S, E), 1)
@@ -249,6 +257,8 @@
 
     field[3] = jnp.zeros((S, E), jnp.float32)
     first = halo(0)
+    pl.semaphore_wait(seen_z, len(line_z))
+    tell(seen_x, line_x)
     turned[0] = field[0].T
     apply(0, first)
     second = halo(1)
@@ -262,6 +272,7 @@
     def total(u, v):
         return jnp.sum((u * v).reshape(S // 8, 8, E), axis=0)
 
+    pl.semaphore_wait(seen_x, len(line_x))
     k0, k1, k2 = field[0], field[1], field[2]
     z1, z2 = aside(k1), aside(k2)
     sums = [
@@ -353,6 +364,8 @@
             pltpu.SemaphoreType.DMA((2, moves)),
             pltpu.SemaphoreType.DMA((nx * nz * nt,)),
             pltpu.SemaphoreType.DMA((nx * nz * nt,)),
+            pltpu.SemaphoreType.REGULAR,
+            pltpu.SemaphoreType.REGULAR,
         ],
         compiler_params=pltpu.CompilerParams(
             collective_id=0, has_side_effects=True, vmem_limit_bytes=56 * 1024 * 1024

time: 24.2 us -> 24.3 us (level)
  no operation moved by 1% of the time
where the time goes in v1:
time: 24.3 us; the launch traced here: 24.2 us
  Pallas kernels  23.5 us (97%)
  between operations  0.64 us (3%)
    pallas_call x1, Pallas kernels, shards(): pl.pallas_call(functools.partial(kernel, sizes), out_shape=(held, held),...  22.9 us
    pallas_call x1, Pallas kernels, shards(): pl.pallas_call(deliver, out_shape=(out, out), in_specs=[pl.BlockSpec(memo...  0.66 us

profile of v1, /device:TPU:0, one launch (start us, length us, event | category | flops | bytes accessed | tf_op | source)
XLA Modules:
  0.0 24.2 jit_solution(13101222058955989494)
XLA Ops:
  0.6 22.9 %shard_map.41 = (f32[1,1,1,128,128]{4,3,2,1,0:T(8,128)S(1)}, f32[1,1,1,128,128]{4,3,2,1,0:T(8,128)S(1)}) custom-call(f32[1,1,1,128,128]{4,3,2,1,0:T(8,128)} %b_hbm.1, f32[1,1,1,9,2,32,32,128]{7,6,5,4,3,2,1,0:T(8,128)} %l_hbm.1), custom_call_target="tpu_custom_call" | custom-call | tf_op jit(solution)/shard_map/pallas_call | solution.py:346
  23.5 0.7 %shard_map.42 = (f32[1,1,1,128,128]{4,3,2,1,0:T(8,128)}, f32[1,1,1,128,128]{4,3,2,1,0:T(8,128)}) custom-call(f32[1,1,1,128,128]{4,3,2,1,0:T(8,128)S(1)} %get-tuple-element.4.a_ref, f32[1,1,1,128,128]{4,3,2,1,0:T(8,128)S(1)} %get-tuple-element.5.b_ref), custom_call_target="tpu_custom_call" | custom-call | tf_op jit(solution)/shard_map/pallas_call | solution.py:374

commit v2 on v0

v2 whole, which is shorter than its diff:
```python
import functools

import jax
import jax.numpy as jnp
from jax import lax
from jax.experimental import pallas as pl
from jax.experimental.pallas import tpu as pltpu
from jax.sharding import PartitionSpec as P

DOF = 32
RHS = 2
NY = 8
CZ = 2
CT = 8
S = 128
E = 128
MESH = pl.DeviceIdType.MESH

mass_shift = 4.0
epsilon = 1e-06


def cmul(a, b):
    return (a[0] * b[0] - a[1] * b[1], a[0] * b[1] + a[1] * b[0])


def conj(a):
    return (a[0], -a[1])


def cadd(a, b):
    return (a[0] + b[0], a[1] + b[1])


def csub(a, b):
    return (a[0] - b[0], a[1] - b[1])


def scale(a, x):
    return (a[0] * x, a[1] * x)


def size2(a):
    return a[0] * a[0] + a[1] * a[1]


def coefficients(g00, g11, g22, g01, g02, g12):
    beta2 = g00 + epsilon
    beta = jnp.sqrt(beta2)
    inv_beta2 = 1.0 / beta2
    h00 = scale((mass_shift * g00 + g01[0], g01[1]), inv_beta2)
    a = (mass_shift - h00[0], -h00[1])
    left = g11 + size2(a) * g00 + 2.0 * cmul(conj(a), g01)[0]
    h10_2 = jnp.maximum(left, 0.0) * inv_beta2 + epsilon
    h10 = jnp.sqrt(h10_2)
    a4 = (a[0] + mass_shift, a[1])
    a_4 = scale(a, mass_shift)
    top = cadd(cadd(g02, cmul(a4, g01)), scale(a_4, g00))
    h01 = scale(top, inv_beta2 / h10)
    low = cadd(cadd(g12, scale(a4, g11)), cmul(a_4, conj(g01)))
    h11 = scale(cadd(low, cmul(conj(a), top)), inv_beta2 / h10_2)
    p = csub(a4, h11)
    q = csub(csub(a_4, scale(h01, h10)), cmul(h11, a))
    left = g22 + size2(p) * g11 + size2(q) * g00
    left = left + 2.0 * (
        cmul(p, conj(g12))[0] + cmul(q, conj(g02))[0] + cmul(cmul(conj(q), p), g01)[0]
    )
    h21_2 = jnp.maximum(left, 0.0) * (inv_beta2 / h10_2) + epsilon
    m00 = size2(h00) + h10_2
    m01 = cadd(cmul(conj(h00), h01), scale(h11, h10))
    m11 = size2(h01) + size2(h11) + h21_2
    t0 = scale(conj(h00), beta)
    t1 = scale(conj(h01), beta)
    inv_l0 = 1.0 / jnp.sqrt(m00)
    l10 = scale(conj(m01), inv_l0)
    f0 = scale(t0, inv_l0)
    inv_d = 1.0 / (m11 - size2(l10))
    y1 = scale(csub(t1, cmul(l10, f0)), inv_d)
    y0 = scale(csub(f0, cmul(conj(l10), y1)), inv_l0)
    inv_beta = 1.0 / beta
    wb = scale(y1, inv_beta / h10)
    wa = cadd(scale(y0, inv_beta), cmul(wb, a))
    return wa, wb


def kernel(
    sizes, b_hbm, l_hbm, sol_ref, res_ref,
    links, edge_links, field, kv, turned, xbuf, zbuf, zpack, tbuf, tpack, acc, red,
    b_sem, l_sem, sent, got, got_sum, seen_z, seen_x,
):
    nx, nz, nt = sizes
    total_count = nx * nz * nt
    ix, iz, it = lax.axis_index("xy"), lax.axis_index("gz"), lax.axis_index("ta")
    here = (ix * nz + iz) * nt + it
    groups = DOF // 8
    ways = 2 if nx > 2 else 1

    def step(axis_value, by, count):
        return lax.rem(axis_value + (by + count), count)

    def at(x, z, t):
        return (x, z, t)

    line_x = [at(step(ix, d, nx), iz, it) for d in range(1, nx)]
    line_z = [at(ix, step(iz, d, nz), it) for d in range(1, nz)]
    line_t = [at(ix, iz, step(it, d, nt)) for d in range(1, nt)]

    def tell(sem, devices):
        for device in devices:
            pl.semaphore_signal(sem, inc=1, device_id=device, device_id_type=MESH)

    def remote(source, target, send_sem, recv_sem, device):
        return pltpu.make_async_remote_copy(
            src_ref=source, dst_ref=target, send_sem=send_sem, recv_sem=recv_sem,
            device_id=device, device_id_type=MESH,
        )

    barrier = pltpu.get_barrier_semaphore()
    tell(barrier, line_t + line_z + line_x)

    b_copy = pltpu.make_async_copy(b_hbm.at[0, 0, 0], field.at[0], b_sem)
    b_copy.start()
    l_copies = {}
    for number, (k, count) in enumerate(((0, 1), (3, 2), (7, 2), (5, 2), (1, 2))):
        part = pl.ds(k, count)
        l_copies[k] = pltpu.make_async_copy(l_hbm.at[0, 0, 0, part], links.at[part], l_sem.at[number])
        l_copies[k].start()

    lane = lax.broadcasted_iota(jnp.int32, (8, 128), 1)
    row8 = lax.broadcasted_iota(jnp.int32, (8, 128), 0)
    in_t = lane % CT
    in_z = (lane // CT) % CZ
    odd = lane % 2 == 1

    def rolled(x, by):
        return pltpu.roll(x, by % S, 1) if by % S else x

    def seat(j):
        return (in_t == 2 * j) | (in_t == (2 * j + CT - 1) % CT)

    seats = [seat(j) for j in range(groups)]

    def tiles(ref, first, count):
        return [ref[pl.ds(first + 8 * j, 8), :] for j in range(count)]

    def halo(n):
        mine = kv.at[n]
        for i in range(2 * RHS):
            rows = tiles(mine, i * DOF, groups)
            packed = None
            for j in range(groups):
                part = jnp.where(odd, rolled(rows[j], 2 * j + CT - 1), rolled(rows[j], 2 * j - CT + 1))
                packed = part if packed is None else jnp.where(seats[j], part, packed)
            tpack[n, pl.ds(8 * i, 8), :] = packed
        for way in (0, 1):
            by = 1 if way else -1
            remote(tpack.at[n], tbuf.at[n, way], sent.at[0], got.at[n, 0], at(ix, iz, step(it, by, nt))).start()
        half = RHS * DOF
        for j in range(half // 8):
            a = mine[pl.ds(8 * j, 8), :]
            b = mine[pl.ds(half + 8 * j, 8), :]
            zpack[n, 0, pl.ds(8 * j, 8), :] = jnp.where(in_z == 0, a, rolled(b, CT))
            zpack[n, 1, pl.ds(8 * j, 8), :] = jnp.where(in_z == 0, rolled(a, -CT), b)
        for way in (0, 1):
            by = 1 if way else -1
            remote(zpack.at[n, way], zbuf.at[n, way], sent.at[1], got.at[n, 1], at(ix, step(iz, by, nz), it)).start()
        for way in range(ways):
            by = 1 if way else -1
            remote(mine, xbuf.at[n, way], sent.at[2], got.at[n, 2], at(step(ix, by, nx), iz, it)).start()

    def receive(n, kind, ref):
        remote(ref, ref, sent.at[kind], got.at[n, kind], (ix, iz, it)).wait_recv()

    def products(passes, fresh, merge=False, final=False):
        def block(c0):
            sums = [[None] * (3 * RHS) for _ in range(4)]
            for link, near in passes:
                for j in range(groups):
                    rows = pl.ds(8 * j, 8)
                    vs = []
                    for r in range(RHS):
                        vr = near[pl.ds(2 * r * DOF + 8 * j, 8), :]
                        vi = near[pl.ds((2 * r + 1) * DOF + 8 * j, 8), :]
                        vs += [vr, vi, vr + vi]
                    for q in range(4):
                        c = c0 + q
                        lr = links[link, 0, c, rows, :]
                        li = links[link, 1, c, rows, :]
                        if merge:
                            lr = lr + links[link + 1, 0, c, rows, :]
                            li = li + links[link + 1, 1, c, rows, :]
                            links[link, 0, c, rows, :] = lr
                            links[link, 1, c, rows, :] = li
                        ls = (lr, li, lr + li)
                        for m in range(3 * RHS):
                            x = ls[m % 3] * vs[m]
                            sums[q][m] = x if sums[q][m] is None else sums[q][m] + x
            out = []
            for q in range(4):
                parts = []
                for r in range(RHS):
                    rr, ii, both = sums[q][3 * r : 3 * r + 3]
                    parts += [rr - ii, both - (rr + ii)]
                if not fresh:
                    parts = [acc[i, c0 + q] + parts[i] for i in range(2 * RHS)]
                out.append(parts)
            return out

        def body(step_number, carry):
            if final:
                c0 = step_number * 8
                out = block(c0) + block(c0 + 4)
                for i in range(2 * RHS):
                    rows = pl.ds(pl.multiple_of(i * DOF + c0, 8), 8)
                    turned[0, rows, :] = fold([out[q][i] for q in range(8)])
            else:
                c0 = step_number * 4
                out = block(c0)
                for q in range(4):
                    for i in range(2 * RHS):
                        acc[i, c0 + q] = out[q][i]
            return carry

        lax.fori_loop(0, DOF // (8 if final else 4), body, 0)

    def split_z():
        def body(c, carry):
            for p in range(2):
                for j in range(groups):
                    rows = pl.ds(8 * j, 8)
                    up, down = links[5, p, c, rows, :], links[6, p, c, rows, :]
                    links[5, p, c, rows, :] = jnp.where(in_z == 0, up, down)
                    links[6, p, c, rows, :] = jnp.where(in_z == 0, down, up)
            return carry

        lax.fori_loop(0, DOF, body, 0, unroll=2)

    def pack_edges():
        last = in_t == CT - 1

        def body(c, carry):
            for p in range(2):
                packed = None
                for j in range(groups):
                    rows = pl.ds(8 * j, 8)
                    part = rolled(jnp.where(last, links[7, p, c, rows, :], links[8, p, c, rows, :]), 2 * j)
                    packed = part if packed is None else jnp.where(seats[j], part, packed)
                edge_links[p, c] = packed
            return carry

        lax.fori_loop(0, DOF, body, 0, unroll=8)

    low4, low2, low1 = row8 < 4, row8 % 4 < 2, row8 % 2 < 1

    def fold(xs):
        ys = [
            jnp.where(low4, xs[i], xs[i + 4]) + pltpu.roll(jnp.where(low4, xs[i + 4], xs[i]), 4, 0)
            for i in range(4)
        ]
        zs = [
            jnp.where(low2, ys[i] + pltpu.roll(ys[i], 6, 0), ys[i + 2] + pltpu.roll(ys[i + 2], 2, 0))
            for i in range(2)
        ]
        return jnp.where(low1, zs[0] + pltpu.roll(zs[0], 7, 0), zs[1] + pltpu.roll(zs[1], 1, 0))

    def shift(n):
        mine = kv.at[n]
        for j in range(E // 8):
            rows = pl.ds(8 * j, 8)
            own = mine[rows, :]
            turned[0, rows, :] = rolled(own, -CZ * CT)
            turned[1, rows, :] = rolled(own, CZ * CT)
            turned[2, rows, :] = jnp.where(in_z == 0, rolled(own, -CT), rolled(own, CT))
            turned[3, rows, :] = jnp.where(in_t == CT - 1, 0.0, rolled(own, -1))
            turned[4, rows, :] = jnp.where(in_t == 0, 0.0, rolled(own, 1))

    local = ((0, None), (3, 0), (4, 1), (7, 3), (8, 4), (5, 2))

    def apply(n):
        shift(n)
        terms = [(link, kv.at[n] if near is None else turned.at[near]) for link, near in local]
        if n == 0:
            l_copies[0].wait()
            l_copies[3].wait()
            products(terms[:3], True)
            l_copies[7].wait()
            products(terms[3:5], False)
            pack_edges()
            l_copies[5].wait()
            split_z()
            products(terms[5:], False)
            pl.semaphore_wait(seen_z, len(line_z))
            tell(seen_x, line_x)
            l_copies[1].wait()
        else:
            products(terms, True)
            early()
        receive(n, 2, xbuf.at[n, pl.ds(0, ways)])
        if nx > 2:
            products(((1, xbuf.at[n, 0]), (2, xbuf.at[n, 1])), False)
        else:
            products(((1, xbuf.at[n, 0]),), False, n == 0)
        receive(n, 1, zbuf.at[n])
        half = RHS * DOF
        for j in range(half // 8):
            p0 = zbuf[n, 0, pl.ds(8 * j, 8), :]
            p1 = zbuf[n, 1, pl.ds(8 * j, 8), :]
            turned[2, pl.ds(8 * j, 8), :] = jnp.where(in_z == 0, p1, rolled(p0, CT))
            turned[2, pl.ds(half + 8 * j, 8), :] = jnp.where(in_z == 0, rolled(p1, -CT), p0)
        products(((6, turned.at[2]),), False, final=True)
        receive(n, 0, tbuf.at[n])
        vs = [
            jnp.where(odd, tbuf[n, 0, pl.ds(8 * i, 8), :], tbuf[n, 1, pl.ds(8 * i, 8), :])
            for i in range(4)
        ]
        for c in range(0, DOF, 8):
            parts = [[] for _ in range(4)]
            for j in range(8):
                lr, li = edge_links[0, c + j], edge_links[1, c + j]
                for r in range(RHS):
                    vr, vi = vs[2 * r], vs[2 * r + 1]
                    parts[2 * r].append(lr * vr - li * vi)
                    parts[2 * r + 1].append(lr * vi + li * vr)
            for i in range(4):
                d = fold(parts[i])
                d = d + rolled(d, -2)
                d = d + rolled(d, -4)
                rows = pl.ds(i * DOF + c, 8)
                kv[n + 1, rows, :] = turned[0, rows, :] + jnp.where(seats[0], d, 0.0)

    def dots(a, b, both):
        out = []
        for r in range(RHS):
            re = im = None
            for j in range(groups):
                ar, ai = (a[pl.ds((2 * r + p) * DOF + 8 * j, 8), :] for p in range(2))
                br, bi = (b[pl.ds((2 * r + p) * DOF + 8 * j, 8), :] for p in range(2))
                x = ar * br + ai * bi
                re = x if re is None else re + x
                if both:
                    x = ar * bi - ai * br
                    im = x if im is None else im + x
            out.append((re, im) if both else (re,))
        return out

    def lane_sums(x):
        return jnp.broadcast_to(jnp.sum(x, axis=1, keepdims=True), (8, 128))

    def early():
        d00, d11, d01 = dots(kv.at[0], kv.at[0], False), dots(kv.at[1], kv.at[1], False), dots(kv.at[0], kv.at[1], True)
        sums = lane_sums(fold([x for r in range(RHS) for x in d00[r] + d11[r] + d01[r]]))
        acc_row = jnp.where(lane == row8, sums, 0.0)
        field[4, pl.ds(0, 8), :] = acc_row

    b_copy.wait()
    kv[0] = field[0].T
    pl.semaphore_wait(barrier, len(line_t) + len(line_z) + len(line_x))
    halo(0)
    tell(seen_z, line_z)
    apply(0)
    halo(1)
    apply(1)

    d02, d12, d22 = dots(kv.at[0], kv.at[2], True), dots(kv.at[1], kv.at[2], True), dots(kv.at[2], kv.at[2], False)
    sums = lane_sums(fold([x for r in range(RHS) for x in d02[r] + d12[r]]))
    a, b = d22[0][0], d22[1][0]
    norms = lane_sums(jnp.where(low4, a + pltpu.roll(a, 4, 0), b + pltpu.roll(b, 4, 0)))
    mine = field[4, pl.ds(0, 8), :] + jnp.where(lane == 8 + row8, sums, 0.0)
    mine = mine + jnp.where(lane == 16 + row8 // 4, norms, 0.0)
    pl.semaphore_wait(seen_x, len(line_x))
    red[here] = jnp.sum(mine, axis=0, keepdims=True)
    for number in range(total_count - 1):
        other = number + jnp.where(here <= number, 1, 0)
        plane = lax.div(other, nt)
        device = (lax.div(plane, nz), lax.rem(plane, nz), lax.rem(other, nt))
        remote(red.at[here], red.at[here], sent.at[3], got_sum, device).start()

    in_p = (lax.broadcasted_iota(jnp.int32, (S, E), 1) // DOF) % 2

    def aside(v):
        return jnp.where(in_p == 0, pltpu.roll(v, E - DOF, 1), -pltpu.roll(v, DOF, 1))

    k1, k2 = kv[1].T, kv[2].T
    field[1] = k1
    field[2] = k2
    turned[0] = aside(field[0])
    turned[1] = aside(k1)
    turned[2] = aside(k2)
    for kind, ref in ((0, tbuf), (1, zbuf), (2, xbuf.at[:, pl.ds(0, ways)])):
        remote(ref, ref, sent.at[kind], got_sum, (ix, iz, it)).wait_send()

    others = red.at[pl.ds(0, total_count - 1)]
    remote(others, others, sent.at[3], got_sum, (ix, iz, it)).wait_recv()
    value = jnp.broadcast_to(jnp.sum(red[...], axis=0), (8, 128))
    first_half = lane < 2 * DOF

    def pick(place):
        return [jnp.sum(jnp.where(lane == place + by * r, value, 0.0), axis=1, keepdims=True) for r, by in ((0, 0), (1, 4))]

    place = (row8 // 4) * 8 + row8 % 4
    low, high = pick(place)
    gram = jnp.where(first_half, low, high)
    low, _ = pick(16 + row8 * 0)
    high, _ = pick(17 + row8 * 0)
    g22 = jnp.where(first_half, low, high)[0:1]
    g = [gram[i : i + 1] for i in range(8)]
    wa, wb = coefficients(g[0], g[1], g22, (g[2], g[3]), (g[4], g[5]), (g[6], g[7]))

    def weighted(w, v, z):
        return w[0] * v - w[1] * z

    k0, k1, k2 = field[0], field[1], field[2]
    z0, z1, z2 = turned[0], turned[1], turned[2]
    sol = weighted(wa, k0, z0) + weighted(wb, k1, z1)
    image = weighted(wa, k1, z1) + weighted(wb, k2, z2)
    sol_ref[0, 0, 0] = sol
    res_ref[0, 0, 0] = k0 - mass_shift * sol - image
    remote(others, others, sent.at[3], got_sum, (ix, iz, it)).wait_send()


def deliver(a_ref, b_ref, sol_ref, res_ref):
    sol_ref[...] = a_ref[...]
    res_ref[...] = b_ref[...]


def shards(sizes, right_side, link_blocks):
    nx, nz, nt = sizes
    out = jax.ShapeDtypeStruct(right_side.shape, jnp.float32)
    f32 = jnp.float32
    held = pltpu.VMEM(right_side.shape, f32)
    results = pl.pallas_call(
        functools.partial(kernel, sizes),
        out_shape=(held, held),
        in_specs=[pl.BlockSpec(memory_space=pl.ANY)] * 2,
        out_specs=(pl.BlockSpec(memory_space=pltpu.VMEM),) * 2,
        scratch_shapes=[
            pltpu.VMEM((9, 2, DOF, DOF, S), f32),
            pltpu.VMEM((2, DOF, 8, S), f32),
            pltpu.VMEM((5, S, E), f32),
            pltpu.VMEM((3, E, S), f32),
            pltpu.VMEM((5, E, S), f32),
            pltpu.VMEM((2, 2 if nx > 2 else 1, E, S), f32),
            pltpu.VMEM((2, 2, RHS * DOF, S), f32),
            pltpu.VMEM((2, 2, RHS * DOF, S), f32),
            pltpu.VMEM((2, 2, 2 * RHS * 8, S), f32),
            pltpu.VMEM((2, 2 * RHS * 8, S), f32),
            pltpu.VMEM((4, DOF, 8, S), f32),
            pltpu.VMEM((nx * nz * nt, 1, 128), f32),
            pltpu.SemaphoreType.DMA,
            pltpu.SemaphoreType.DMA((5,)),
            pltpu.SemaphoreType.DMA((4,)),
            pltpu.SemaphoreType.DMA((2, 3)),
            pltpu.SemaphoreType.DMA,
            pltpu.SemaphoreType.REGULAR,
            pltpu.SemaphoreType.REGULAR,
        ],
        compiler_params=pltpu.CompilerParams(
            collective_id=0, has_side_effects=True, vmem_limit_bytes=56 * 1024 * 1024
        ),
    )(right_side, link_blocks)
    return pl.pallas_call(
        deliver,
        out_shape=(out, out),
        in_specs=[pl.BlockSpec(memory_space=pltpu.VMEM)] * 2,
        out_specs=(pl.BlockSpec(memory_space=pltpu.VMEM),) * 2,
    )(*[pltpu.with_memory_space_constraint(x, pltpu.VMEM) for x in results])


def solution(mesh):
    sizes = tuple(mesh.shape[name] for name in ("xy", "gz", "ta"))
    return jax.shard_map(
        functools.partial(shards, sizes),
        mesh=mesh,
        in_specs=(
            P("xy", "gz", "ta", None, None),
            P("xy", "gz", "ta", None, None, None, None, None),
        ),
        out_specs=(P("xy", "gz", "ta", None, None), P("xy", "gz", "ta", None, None)),
        check_vma=False,
    )
```

time: 24.2 us -> 23.1 us (0.955)
  Pallas kernels: 23.4 us -> 22.3 us
    pallas_call x1, Pallas kernels: 22.8 us -> 21.7 us  [shards(): pl.pallas_call(functools.partial(kernel, sizes), out_shape=(held, held),...]
where the time goes in v2:
time: 23.1 us; the launch traced here: 23 us
  Pallas kernels  22.3 us (97%)
  between operations  0.64 us (3%)
    pallas_call x1, Pallas kernels, shards(): pl.pallas_call(functools.partial(kernel, sizes), out_shape=(held, held),...  21.7 us
    pallas_call x1, Pallas kernels, shards(): pl.pallas_call(deliver, out_shape=(out, out), in_specs=[pl.BlockSpec(memo...  0.66 us

profile of v2, /device:TPU:0, one launch (start us, length us, event | category | flops | bytes accessed | tf_op | source)
XLA Modules:
  0.0 23.0 jit_solution(885832875532651393)
XLA Ops:
  0.6 21.7 %shard_map.41 = (f32[1,1,1,128,128]{4,3,2,1,0:T(8,128)S(1)}, f32[1,1,1,128,128]{4,3,2,1,0:T(8,128)S(1)}) custom-call(f32[1,1,1,128,128]{4,3,2,1,0:T(8,128)} %b_hbm.1, f32[1,1,1,9,2,32,32,128]{7,6,5,4,3,2,1,0:T(8,128)} %l_hbm.1), custom_call_target="tpu_custom_call" | custom-call | tf_op jit(solution)/shard_map/pallas_call | solution.py:431
  22.3 0.7 %shard_map.42 = (f32[1,1,1,128,128]{4,3,2,1,0:T(8,128)}, f32[1,1,1,128,128]{4,3,2,1,0:T(8,128)}) custom-call(f32[1,1,1,128,128]{4,3,2,1,0:T(8,128)S(1)} %get-tuple-element.4.a_ref, f32[1,1,1,128,128]{4,3,2,1,0:T(8,128)S(1)} %get-tuple-element.5.b_ref), custom_call_target="tpu_custom_call" | custom-call | tf_op jit(solution)/shard_map/pallas_call | solution.py:461

commit v3 on v2

--- a/solution.py
+++ b/solution.py
@@ -1,4 +1,5 @@
 import functools
+import itertools
 
 import jax
 import jax.numpy as jnp
@@ -124,7 +125,7 @@
     for number, (k, count) in enumerate(((0, 1), (3, 2), (7, 2), (5, 2), (1, 2))):
         part = pl.ds(k, count)
         l_copies[k] = pltpu.make_async_copy(l_hbm.at[0, 0, 0, part], links.at[part], l_sem.at[number])
-        l_copies[k].start()
+        l_copies[k].start(priority=1)
 
     lane = lax.broadcasted_iota(jnp.int32, (8, 128), 1)
     row8 = lax.broadcasted_iota(jnp.int32, (8, 128), 0)
@@ -369,11 +370,11 @@
     mine = mine + jnp.where(lane == 16 + row8 // 4, norms, 0.0)
     pl.semaphore_wait(seen_x, len(line_x))
     red[here] = jnp.sum(mine, axis=0, keepdims=True)
-    for number in range(total_count - 1):
-        other = number + jnp.where(here <= number, 1, 0)
-        plane = lax.div(other, nt)
-        device = (lax.div(plane, nz), lax.rem(plane, nz), lax.rem(other, nt))
-        remote(red.at[here], red.at[here], sent.at[3], got_sum, device).start()
+    for x, z, t in itertools.product(range(nx), range(nz), range(nt)):
+
+        @pl.when((x * nz + z) * nt + t != here)
+        def _():
+            remote(red.at[here], red.at[here], sent.at[3], got_sum, (x, z, t)).start()
 
     in_p = (lax.broadcasted_iota(jnp.int32, (S, E), 1) // DOF) % 2
 

time: 23.1 us -> 20.5 us (0.89)
  Pallas kernels: 22.3 us -> 19.7 us
    pallas_call x1, Pallas kernels: 21.7 us -> 19.1 us  [shards(): pl.pallas_call(functools.partial(kernel, sizes), out_shape=(held, held),...]
where the time goes in v3:
time: 20.5 us; the launch traced here: 20.4 us
  Pallas kernels  19.7 us (96%)
  between operations  0.64 us (3%)
    pallas_call x1, Pallas kernels, shards(): pl.pallas_call(functools.partial(kernel, sizes), out_shape=(held, held),...  19.1 us
    pallas_call x1, Pallas kernels, shards(): pl.pallas_call(deliver, out_shape=(out, out), in_specs=[pl.BlockSpec(memo...  0.66 us

profile of v3, /device:TPU:0, one launch (start us, length us, event | category | flops | bytes accessed | tf_op | source)
XLA Modules:
  0.0 20.4 jit_solution(4464458106972360115)
XLA Ops:
  0.6 19.1 %shard_map.41 = (f32[1,1,1,128,128]{4,3,2,1,0:T(8,128)S(1)}, f32[1,1,1,128,128]{4,3,2,1,0:T(8,128)S(1)}) custom-call(f32[1,1,1,128,128]{4,3,2,1,0:T(8,128)} %b_hbm.1, f32[1,1,1,9,2,32,32,128]{7,6,5,4,3,2,1,0:T(8,128)} %l_hbm.1), custom_call_target="tpu_custom_call" | custom-call | tf_op jit(solution)/shard_map/pallas_call | solution.py:432
  19.7 0.7 %shard_map.42 = (f32[1,1,1,128,128]{4,3,2,1,0:T(8,128)}, f32[1,1,1,128,128]{4,3,2,1,0:T(8,128)}) custom-call(f32[1,1,1,128,128]{4,3,2,1,0:T(8,128)S(1)} %get-tuple-element.4.a_ref, f32[1,1,1,128,128]{4,3,2,1,0:T(8,128)S(1)} %get-tuple-element.5.b_ref), custom_call_target="tpu_custom_call" | custom-call | tf_op jit(solution)/shard_map/pallas_call | solution.py:462

commit v4 on v3

--- a/solution.py
+++ b/solution.py
@@ -116,11 +116,12 @@
             device_id=device, device_id_type=MESH,
         )
 
+    b_copy = pltpu.make_async_copy(b_hbm.at[0, 0, 0], field.at[0], b_sem)
+    b_copy.start()
+
     barrier = pltpu.get_barrier_semaphore()
     tell(barrier, line_t + line_z + line_x)
 
-    b_copy = pltpu.make_async_copy(b_hbm.at[0, 0, 0], field.at[0], b_sem)
-    b_copy.start()
     l_copies = {}
     for number, (k, count) in enumerate(((0, 1), (3, 2), (7, 2), (5, 2), (1, 2))):
         part = pl.ds(k, count)
@@ -143,6 +144,10 @@
 
     def tiles(ref, first, count):
         return [ref[pl.ds(first + 8 * j, 8), :] for j in range(count)]
+
+    def z_rows(h):
+        count = groups // 2
+        return [(p, h * count + d, (p * count + d) * 8) for p in range(2) for d in range(count)]
 
     def halo(n):
         mine = kv.at[n]
@@ -156,27 +161,29 @@
         for way in (0, 1):
             by = 1 if way else -1
             remote(tpack.at[n], tbuf.at[n, way], sent.at[0], got.at[n, 0], at(ix, iz, step(it, by, nt))).start()
-        half = RHS * DOF
-        for j in range(half // 8):
-            a = mine[pl.ds(8 * j, 8), :]
-            b = mine[pl.ds(half + 8 * j, 8), :]
-            zpack[n, 0, pl.ds(8 * j, 8), :] = jnp.where(in_z == 0, a, rolled(b, CT))
-            zpack[n, 1, pl.ds(8 * j, 8), :] = jnp.where(in_z == 0, rolled(a, -CT), b)
-        for way in (0, 1):
-            by = 1 if way else -1
-            remote(zpack.at[n, way], zbuf.at[n, way], sent.at[1], got.at[n, 1], at(ix, step(iz, by, nz), it)).start()
+        for h in range(2):
+            for p, dj, row in z_rows(h):
+                a = mine[pl.ds(p * DOF + 8 * dj, 8), :]
+                b = mine[pl.ds((2 + p) * DOF + 8 * dj, 8), :]
+                zpack[n, h, 0, pl.ds(row, 8), :] = jnp.where(in_z == 0, a, rolled(b, CT))
+                zpack[n, h, 1, pl.ds(row, 8), :] = jnp.where(in_z == 0, rolled(a, -CT), b)
+            for way in (0, 1):
+                by = 1 if way else -1
+                remote(
+                    zpack.at[n, h, way], zbuf.at[n, h, way], sent.at[1], got.at[n, 2 + h], at(ix, step(iz, by, nz), it)
+                ).start()
         for way in range(ways):
             by = 1 if way else -1
-            remote(mine, xbuf.at[n, way], sent.at[2], got.at[n, 2], at(step(ix, by, nx), iz, it)).start()
+            remote(mine, xbuf.at[n, way], sent.at[2], got.at[n, 1], at(step(ix, by, nx), iz, it)).start()
 
     def receive(n, kind, ref):
-        remote(ref, ref, sent.at[kind], got.at[n, kind], (ix, iz, it)).wait_recv()
-
-    def products(passes, fresh, merge=False, final=False):
+        remote(ref, ref, sent.at[0], got.at[n, kind], (ix, iz, it)).wait_recv()
+
+    def products(passes, fresh, merge=False, final=False, span=range(groups)):
         def block(c0):
             sums = [[None] * (3 * RHS) for _ in range(4)]
             for link, near in passes:
-                for j in range(groups):
+                for j in span:
                     rows = pl.ds(8 * j, 8)
                     vs = []
                     for r in range(RHS):
@@ -213,7 +220,7 @@
                 out = block(c0) + block(c0 + 4)
                 for i in range(2 * RHS):
                     rows = pl.ds(pl.multiple_of(i * DOF + c0, 8), 8)
-                    turned[0, rows, :] = fold([out[q][i] for q in range(8)])
+                    turned[0, rows, :] = turned[0, rows, :] + fold([out[q][i] for q in range(8)])
             else:
                 c0 = step_number * 4
                 out = block(c0)
@@ -296,19 +303,24 @@
         else:
             products(terms, True)
             early()
-        receive(n, 2, xbuf.at[n, pl.ds(0, ways)])
+        receive(n, 1, xbuf.at[n, pl.ds(0, ways)])
         if nx > 2:
             products(((1, xbuf.at[n, 0]), (2, xbuf.at[n, 1])), False)
         else:
             products(((1, xbuf.at[n, 0]),), False, n == 0)
-        receive(n, 1, zbuf.at[n])
-        half = RHS * DOF
-        for j in range(half // 8):
-            p0 = zbuf[n, 0, pl.ds(8 * j, 8), :]
-            p1 = zbuf[n, 1, pl.ds(8 * j, 8), :]
-            turned[2, pl.ds(8 * j, 8), :] = jnp.where(in_z == 0, p1, rolled(p0, CT))
-            turned[2, pl.ds(half + 8 * j, 8), :] = jnp.where(in_z == 0, rolled(p1, -CT), p0)
-        products(((6, turned.at[2]),), False, final=True)
+        for h in range(2):
+            receive(n, 2 + h, zbuf.at[n, h])
+            for p, dj, row in z_rows(h):
+                p0 = zbuf[n, h, 0, pl.ds(row, 8), :]
+                p1 = zbuf[n, h, 1, pl.ds(row, 8), :]
+                turned[2, pl.ds(p * DOF + 8 * dj, 8), :] = jnp.where(in_z == 0, p1, rolled(p0, CT))
+                turned[2, pl.ds((2 + p) * DOF + 8 * dj, 8), :] = jnp.where(in_z == 0, rolled(p1, -CT), p0)
+            span = range(h * groups // 2, (h + 1) * groups // 2)
+            products(((6, turned.at[2]),), h == 1, final=h == 1, span=span)
+            if h == 0:
+                for i in range(4):
+                    for c in range(0, DOF, 8):
+                        turned[0, pl.ds(i * DOF + c, 8), :] = fold([acc[i, c + j] for j in range(8)])
         receive(n, 0, tbuf.at[n])
         vs = [
             jnp.where(odd, tbuf[n, 0, pl.ds(8 * i, 8), :], tbuf[n, 1, pl.ds(8 * i, 8), :])
@@ -324,8 +336,7 @@
                     parts[2 * r + 1].append(lr * vi + li * vr)
             for i in range(4):
                 d = fold(parts[i])
-                d = d + rolled(d, -2)
-                d = d + rolled(d, -4)
+                d = (d + rolled(d, -2)) + (rolled(d, -4) + rolled(d, -6))
                 rows = pl.ds(i * DOF + c, 8)
                 kv[n + 1, rows, :] = turned[0, rows, :] + jnp.where(seats[0], d, 0.0)
 
@@ -441,8 +452,8 @@
             pltpu.VMEM((3, E, S), f32),
             pltpu.VMEM((5, E, S), f32),
             pltpu.VMEM((2, 2 if nx > 2 else 1, E, S), f32),
-            pltpu.VMEM((2, 2, RHS * DOF, S), f32),
-            pltpu.VMEM((2, 2, RHS * DOF, S), f32),
+            pltpu.VMEM((2, 2, 2, DOF, S), f32),
+            pltpu.VMEM((2, 2, 2, DOF, S), f32),
             pltpu.VMEM((2, 2, 2 * RHS * 8, S), f32),
             pltpu.VMEM((2, 2 * RHS * 8, S), f32),
             pltpu.VMEM((4, DOF, 8, S), f32),
@@ -450,7 +461,7 @@
             pltpu.SemaphoreType.DMA,
             pltpu.SemaphoreType.DMA((5,)),
             pltpu.SemaphoreType.DMA((4,)),
-            pltpu.SemaphoreType.DMA((2, 3)),
+            pltpu.SemaphoreType.DMA((2, 4)),
             pltpu.SemaphoreType.DMA,
             pltpu.SemaphoreType.REGULAR,
             pltpu.SemaphoreType.REGULAR,

time: 20.5 us -> 20.3 us (level)
    pallas_call x1, Pallas kernels: 19.1 us -> 18.8 us  [shards(): pl.pallas_call(functools.partial(kernel, sizes), out_shape=(held, held),...]
where the time goes in v4:
time: 20.3 us; the launch traced here: 20.1 us
  Pallas kernels  19.5 us (96%)
  between operations  0.64 us (3%)
    pallas_call x1, Pallas kernels, shards(): pl.pallas_call(functools.partial(kernel, sizes), out_shape=(held, held),...  18.8 us
    pallas_call x1, Pallas kernels, shards(): pl.pallas_call(deliver, out_shape=(out, out), in_specs=[pl.BlockSpec(memo...  0.66 us

profile of v4, /device:TPU:0, one launch (start us, length us, event | category | flops | bytes accessed | tf_op | source)
XLA Modules:
  0.0 20.1 jit_solution(7919584824304109637)
XLA Ops:
  0.6 18.8 %shard_map.41 = (f32[1,1,1,128,128]{4,3,2,1,0:T(8,128)S(1)}, f32[1,1,1,128,128]{4,3,2,1,0:T(8,128)S(1)}) custom-call(f32[1,1,1,128,128]{4,3,2,1,0:T(8,128)} %b_hbm.1, f32[1,1,1,9,2,32,32,128]{7,6,5,4,3,2,1,0:T(8,128)} %l_hbm.1), custom_call_target="tpu_custom_call" | custom-call | tf_op jit(solution)/shard_map/pallas_call | solution.py:443
  19.5 0.7 %shard_map.42 = (f32[1,1,1,128,128]{4,3,2,1,0:T(8,128)}, f32[1,1,1,128,128]{4,3,2,1,0:T(8,128)}) custom-call(f32[1,1,1,128,128]{4,3,2,1,0:T(8,128)S(1)} %get-tuple-element.4.a_ref, f32[1,1,1,128,128]{4,3,2,1,0:T(8,128)S(1)} %get-tuple-element.5.b_ref), custom_call_target="tpu_custom_call" | custom-call | tf_op jit(solution)/shard_map/pallas_call | solution.py:473

commit v5 on v4

--- a/solution.py
+++ b/solution.py
@@ -86,7 +86,7 @@
 
 def kernel(
     sizes, b_hbm, l_hbm, sol_ref, res_ref,
-    links, edge_links, field, kv, turned, xbuf, zbuf, zpack, tbuf, tpack, acc, red,
+    links, edge_links, z_links, rows, field, kv, turned, xbuf, zbuf, zpack, tbuf, tpack, acc, red,
     b_sem, l_sem, sent, got, got_sum, seen_z, seen_x,
 ):
     nx, nz, nt = sizes
@@ -179,11 +179,11 @@
     def receive(n, kind, ref):
         remote(ref, ref, sent.at[0], got.at[n, kind], (ix, iz, it)).wait_recv()
 
-    def products(passes, fresh, merge=False, final=False, span=range(groups)):
+    def products(passes, fresh, merge=False):
         def block(c0):
             sums = [[None] * (3 * RHS) for _ in range(4)]
             for link, near in passes:
-                for j in span:
+                for j in range(groups):
                     rows = pl.ds(8 * j, 8)
                     vs = []
                     for r in range(RHS):
@@ -215,21 +215,14 @@
             return out
 
         def body(step_number, carry):
-            if final:
-                c0 = step_number * 8
-                out = block(c0) + block(c0 + 4)
+            c0 = step_number * 4
+            out = block(c0)
+            for q in range(4):
                 for i in range(2 * RHS):
-                    rows = pl.ds(pl.multiple_of(i * DOF + c0, 8), 8)
-                    turned[0, rows, :] = turned[0, rows, :] + fold([out[q][i] for q in range(8)])
-            else:
-                c0 = step_number * 4
-                out = block(c0)
-                for q in range(4):
-                    for i in range(2 * RHS):
-                        acc[i, c0 + q] = out[q][i]
+                    acc[i, c0 + q] = out[q][i]
             return carry
 
-        lax.fori_loop(0, DOF // (8 if final else 4), body, 0)
+        lax.fori_loop(0, DOF // 4, body, 0)
 
     def split_z():
         def body(c, carry):
@@ -238,7 +231,7 @@
                     rows = pl.ds(8 * j, 8)
                     up, down = links[5, p, c, rows, :], links[6, p, c, rows, :]
                     links[5, p, c, rows, :] = jnp.where(in_z == 0, up, down)
-                    links[6, p, c, rows, :] = jnp.where(in_z == 0, down, up)
+                    z_links[p, pl.ds(c * (DOF + 1) + 8 * j, 8), :] = jnp.where(in_z == 0, down, up)
             return carry
 
         lax.fori_loop(0, DOF, body, 0, unroll=2)
@@ -253,7 +246,7 @@
                     rows = pl.ds(8 * j, 8)
                     part = rolled(jnp.where(last, links[7, p, c, rows, :], links[8, p, c, rows, :]), 2 * j)
                     packed = part if packed is None else jnp.where(seats[j], part, packed)
-                edge_links[p, c] = packed
+                edge_links[p, pl.ds(pl.multiple_of(8 * c, 8), 8), :] = packed
             return carry
 
         lax.fori_loop(0, DOF, body, 0, unroll=8)
@@ -281,6 +274,23 @@
             turned[2, rows, :] = jnp.where(in_z == 0, rolled(own, -CT), rolled(own, CT))
             turned[3, rows, :] = jnp.where(in_t == CT - 1, 0.0, rolled(own, -1))
             turned[4, rows, :] = jnp.where(in_t == 0, 0.0, rolled(own, 1))
+
+    def row_products(link_at, row_at, steps):
+        sums = [[None] * groups for _ in range(3 * RHS)]
+        for d in steps:
+            vs = [jnp.broadcast_to(row_at(m, d), (8, 128)) for m in range(3 * RHS)]
+            for g in range(groups):
+                lr, li = link_at(0, g, d), link_at(1, g, d)
+                ls = (lr, li, lr + li)
+                for m in range(3 * RHS):
+                    x = ls[m % 3] * vs[m]
+                    sums[m][g] = x if sums[m][g] is None else sums[m][g] + x
+        out = []
+        for r in range(RHS):
+            rr, ii, both = sums[3 * r : 3 * r + 3]
+            out.append([rr[g] - ii[g] for g in range(groups)])
+            out.append([both[g] - (rr[g] + ii[g]) for g in range(groups)])
+        return out
 
     local = ((0, None), (3, 0), (4, 1), (7, 3), (8, 4), (5, 2))
 
@@ -308,37 +318,49 @@
             products(((1, xbuf.at[n, 0]), (2, xbuf.at[n, 1])), False)
         else:
             products(((1, xbuf.at[n, 0]),), False, n == 0)
+        for i in range(4):
+            for c in range(0, DOF, 8):
+                turned[0, pl.ds(i * DOF + c, 8), :] = fold([acc[i, c + j] for j in range(8)])
         for h in range(2):
             receive(n, 2 + h, zbuf.at[n, h])
+            near = {}
             for p, dj, row in z_rows(h):
                 p0 = zbuf[n, h, 0, pl.ds(row, 8), :]
                 p1 = zbuf[n, h, 1, pl.ds(row, 8), :]
-                turned[2, pl.ds(p * DOF + 8 * dj, 8), :] = jnp.where(in_z == 0, p1, rolled(p0, CT))
-                turned[2, pl.ds((2 + p) * DOF + 8 * dj, 8), :] = jnp.where(in_z == 0, rolled(p1, -CT), p0)
-            span = range(h * groups // 2, (h + 1) * groups // 2)
-            products(((6, turned.at[2]),), h == 1, final=h == 1, span=span)
-            if h == 0:
-                for i in range(4):
-                    for c in range(0, DOF, 8):
-                        turned[0, pl.ds(i * DOF + c, 8), :] = fold([acc[i, c + j] for j in range(8)])
+                near[0, p, dj] = jnp.where(in_z == 0, p1, rolled(p0, CT))
+                near[1, p, dj] = jnp.where(in_z == 0, rolled(p1, -CT), p0)
+            for r, p, dj in near:
+                rows[3 * r + p, pl.ds(8 * dj, 8), :] = near[r, p, dj]
+                if p == 0:
+                    rows[3 * r + 2, pl.ds(8 * dj, 8), :] = near[r, 0, dj] + near[r, 1, dj]
+            got_z = row_products(
+                lambda p, g, d: z_links[p, pl.ds(8 * g * (DOF + 1) + d, 8, stride=DOF + 1), :],
+                lambda m, d: rows[m, pl.ds(d, 1), :],
+                range(h * DOF // 2, (h + 1) * DOF // 2),
+            )
+            for i in range(4):
+                for g in range(groups):
+                    place = pl.ds(i * DOF + 8 * g, 8)
+                    turned[0, place, :] = turned[0, place, :] + got_z[i][g]
         receive(n, 0, tbuf.at[n])
-        vs = [
-            jnp.where(odd, tbuf[n, 0, pl.ds(8 * i, 8), :], tbuf[n, 1, pl.ds(8 * i, 8), :])
-            for i in range(4)
-        ]
-        for c in range(0, DOF, 8):
-            parts = [[] for _ in range(4)]
-            for j in range(8):
-                lr, li = edge_links[0, c + j], edge_links[1, c + j]
-                for r in range(RHS):
-                    vr, vi = vs[2 * r], vs[2 * r + 1]
-                    parts[2 * r].append(lr * vr - li * vi)
-                    parts[2 * r + 1].append(lr * vi + li * vr)
-            for i in range(4):
-                d = fold(parts[i])
+        for r in range(RHS):
+            vr, vi = (
+                jnp.where(odd, tbuf[n, 0, pl.ds(8 * i, 8), :], tbuf[n, 1, pl.ds(8 * i, 8), :])
+                for i in (2 * r, 2 * r + 1)
+            )
+            for m, v in enumerate((vr, vi, vr + vi)):
+                rows[3 * r + m, pl.ds(DOF, 8), :] = v
+        got_t = row_products(
+            lambda p, g, d: edge_links[p, pl.ds(64 * g + d, 8, stride=8), :],
+            lambda m, d: rows[m, pl.ds(DOF + d, 1), :],
+            range(8),
+        )
+        for i in range(4):
+            for g in range(groups):
+                d = got_t[i][g]
                 d = (d + rolled(d, -2)) + (rolled(d, -4) + rolled(d, -6))
-                rows = pl.ds(i * DOF + c, 8)
-                kv[n + 1, rows, :] = turned[0, rows, :] + jnp.where(seats[0], d, 0.0)
+                place = pl.ds(i * DOF + 8 * g, 8)
+                kv[n + 1, place, :] = turned[0, place, :] + jnp.where(seats[0], d, 0.0)
 
     def dots(a, b, both):
         out = []
@@ -447,7 +469,9 @@
         out_specs=(pl.BlockSpec(memory_space=pltpu.VMEM),) * 2,
         scratch_shapes=[
             pltpu.VMEM((9, 2, DOF, DOF, S), f32),
-            pltpu.VMEM((2, DOF, 8, S), f32),
+            pltpu.VMEM((2, DOF * 8, S), f32),
+            pltpu.VMEM((2, DOF * (DOF + 1), S), f32),
+            pltpu.VMEM((3 * RHS, DOF + 8, S), f32),
             pltpu.VMEM((5, S, E), f32),
             pltpu.VMEM((3, E, S), f32),
             pltpu.VMEM((5, E, S), f32),

time: 20.3 us -> 20.1 us (level)
    pallas_call x1, Pallas kernels: 18.8 us -> 18.6 us  [shards(): pl.pallas_call(functools.partial(kernel, sizes), out_shape=(held, held),...]
where the time goes in v5:
time: 20.1 us; the launch traced here: 19.9 us
  Pallas kernels  19.3 us (96%)
  between operations  0.64 us (3%)
    pallas_call x1, Pallas kernels, shards(): pl.pallas_call(functools.partial(kernel, sizes), out_shape=(held, held),...  18.6 us
    pallas_call x1, Pallas kernels, shards(): pl.pallas_call(deliver, out_shape=(out, out), in_specs=[pl.BlockSpec(memo...  0.66 us

profile of v5, /device:TPU:0, one launch (start us, length us, event | category | flops | bytes accessed | tf_op | source)
XLA Modules:
  0.0 19.9 jit_solution(1967888122075045562)
XLA Ops:
  0.6 18.6 %shard_map.41 = (f32[1,1,1,128,128]{4,3,2,1,0:T(8,128)S(1)}, f32[1,1,1,128,128]{4,3,2,1,0:T(8,128)S(1)}) custom-call(f32[1,1,1,128,128]{4,3,2,1,0:T(8,128)} %b_hbm.1, f32[1,1,1,9,2,32,32,128]{7,6,5,4,3,2,1,0:T(8,128)} %l_hbm.1), custom_call_target="tpu_custom_call" | custom-call | tf_op jit(solution)/shard_map/pallas_call | solution.py:465
  19.2 0.7 %shard_map.42 = (f32[1,1,1,128,128]{4,3,2,1,0:T(8,128)}, f32[1,1,1,128,128]{4,3,2,1,0:T(8,128)}) custom-call(f32[1,1,1,128,128]{4,3,2,1,0:T(8,128)S(1)} %get-tuple-element.4.a_ref, f32[1,1,1,128,128]{4,3,2,1,0:T(8,128)S(1)} %get-tuple-element.5.b_ref), custom_call_target="tpu_custom_call" | custom-call | tf_op jit(solution)/shard_map/pallas_call | solution.py:497

commit v6 on v5

--- a/solution.py
+++ b/solution.py
@@ -122,11 +122,13 @@
     barrier = pltpu.get_barrier_semaphore()
     tell(barrier, line_t + line_z + line_x)
 
-    l_copies = {}
-    for number, (k, count) in enumerate(((0, 1), (3, 2), (7, 2), (5, 2), (1, 2))):
+    for number, k, count in ((0, 0, 1), (0, 3, 2), (1, 7, 2), (1, 5, 2), (2, 1, 2)):
         part = pl.ds(k, count)
-        l_copies[k] = pltpu.make_async_copy(l_hbm.at[0, 0, 0, part], links.at[part], l_sem.at[number])
-        l_copies[k].start(priority=1)
+        pltpu.make_async_copy(l_hbm.at[0, 0, 0, part], links.at[part], l_sem.at[number]).start(priority=1)
+
+    def wait_links(number, count):
+        part = links.at[pl.ds(0, count)]
+        pltpu.make_async_copy(part, part, l_sem.at[number]).wait()
 
     lane = lax.broadcasted_iota(jnp.int32, (8, 128), 1)
     row8 = lax.broadcasted_iota(jnp.int32, (8, 128), 0)
@@ -170,11 +172,11 @@
             for way in (0, 1):
                 by = 1 if way else -1
                 remote(
-                    zpack.at[n, h, way], zbuf.at[n, h, way], sent.at[1], got.at[n, 2 + h], at(ix, step(iz, by, nz), it)
+                    zpack.at[n, h, way], zbuf.at[n, h, way], sent.at[0], got.at[n, 2 + h], at(ix, step(iz, by, nz), it)
                 ).start()
         for way in range(ways):
             by = 1 if way else -1
-            remote(mine, xbuf.at[n, way], sent.at[2], got.at[n, 1], at(step(ix, by, nx), iz, it)).start()
+            remote(mine, xbuf.at[n, way], sent.at[0], got.at[n, 1], at(step(ix, by, nx), iz, it)).start()
 
     def receive(n, kind, ref):
         remote(ref, ref, sent.at[0], got.at[n, kind], (ix, iz, it)).wait_recv()
@@ -298,18 +300,16 @@
         shift(n)
         terms = [(link, kv.at[n] if near is None else turned.at[near]) for link, near in local]
         if n == 0:
-            l_copies[0].wait()
-            l_copies[3].wait()
+            wait_links(0, 3)
             products(terms[:3], True)
-            l_copies[7].wait()
+            wait_links(1, 4)
             products(terms[3:5], False)
             pack_edges()
-            l_copies[5].wait()
             split_z()
             products(terms[5:], False)
             pl.semaphore_wait(seen_z, len(line_z))
             tell(seen_x, line_x)
-            l_copies[1].wait()
+            wait_links(2, 2)
         else:
             products(terms, True)
             early()
@@ -407,24 +407,24 @@
 
         @pl.when((x * nz + z) * nt + t != here)
         def _():
-            remote(red.at[here], red.at[here], sent.at[3], got_sum, (x, z, t)).start()
+            remote(red.at[here], red.at[here], sent.at[1], got_sum, (x, z, t)).start()
 
     in_p = (lax.broadcasted_iota(jnp.int32, (S, E), 1) // DOF) % 2
 
     def aside(v):
         return jnp.where(in_p == 0, pltpu.roll(v, E - DOF, 1), -pltpu.roll(v, DOF, 1))
 
-    k1, k2 = kv[1].T, kv[2].T
-    field[1] = k1
-    field[2] = k2
-    turned[0] = aside(field[0])
-    turned[1] = aside(k1)
-    turned[2] = aside(k2)
-    for kind, ref in ((0, tbuf), (1, zbuf), (2, xbuf.at[:, pl.ds(0, ways)])):
-        remote(ref, ref, sent.at[kind], got_sum, (ix, iz, it)).wait_send()
+    k0, k1, k2 = field[0], kv[1].T, kv[2].T
+    low, high = mass_shift * k0 + k1, mass_shift * k1 + k2
+    for number, v in enumerate((k0, k1, low, high)):
+        if number:
+            field[number] = v
+        turned[number] = aside(v)
+    halo_bytes = links.at[0, 0, pl.ds(0, 2 * (2 + 4 + ways * E // DOF))]
+    remote(halo_bytes, halo_bytes, sent.at[0], got_sum, (ix, iz, it)).wait_send()
 
     others = red.at[pl.ds(0, total_count - 1)]
-    remote(others, others, sent.at[3], got_sum, (ix, iz, it)).wait_recv()
+    remote(others, others, sent.at[1], got_sum, (ix, iz, it)).wait_recv()
     value = jnp.broadcast_to(jnp.sum(red[...], axis=0), (8, 128))
     first_half = lane < 2 * DOF
 
@@ -440,16 +440,14 @@
     g = [gram[i : i + 1] for i in range(8)]
     wa, wb = coefficients(g[0], g[1], g22, (g[2], g[3]), (g[4], g[5]), (g[6], g[7]))
 
-    def weighted(w, v, z):
-        return w[0] * v - w[1] * z
-
-    k0, k1, k2 = field[0], field[1], field[2]
-    z0, z1, z2 = turned[0], turned[1], turned[2]
-    sol = weighted(wa, k0, z0) + weighted(wb, k1, z1)
-    image = weighted(wa, k1, z1) + weighted(wb, k2, z2)
-    sol_ref[0, 0, 0] = sol
-    res_ref[0, 0, 0] = k0 - mass_shift * sol - image
-    remote(others, others, sent.at[3], got_sum, (ix, iz, it)).wait_send()
+    wa, wb = ([jnp.broadcast_to(x, (8, 128)) for x in w] for w in (wa, wb))
+    for j in range(S // 8):
+        rows8 = pl.ds(8 * j, 8)
+        k0, k1, low, high = (field[number, rows8, :] for number in range(4))
+        z0, z1, z_low, z_high = (turned[number, rows8, :] for number in range(4))
+        sol_ref[0, 0, 0, rows8, :] = (wa[0] * k0 - wa[1] * z0) + (wb[0] * k1 - wb[1] * z1)
+        res_ref[0, 0, 0, rows8, :] = k0 - (wa[0] * low - wa[1] * z_low) - (wb[0] * high - wb[1] * z_high)
+    remote(others, others, sent.at[1], got_sum, (ix, iz, it)).wait_send()
 
 
 def deliver(a_ref, b_ref, sol_ref, res_ref):
@@ -483,8 +481,8 @@
             pltpu.VMEM((4, DOF, 8, S), f32),
             pltpu.VMEM((nx * nz * nt, 1, 128), f32),
             pltpu.SemaphoreType.DMA,
-            pltpu.SemaphoreType.DMA((5,)),
-            pltpu.SemaphoreType.DMA((4,)),
+            pltpu.SemaphoreType.DMA((3,)),
+            pltpu.SemaphoreType.DMA((2,)),
             pltpu.SemaphoreType.DMA((2, 4)),
             pltpu.SemaphoreType.DMA,
             pltpu.SemaphoreType.REGULAR,

time: 20.1 us -> 20 us (level)
  no operation moved by 1% of the time
where the time goes in v6:
time: 20 us; the launch traced here: 19.9 us
  Pallas kernels  19.2 us (96%)
  between operations  0.64 us (3%)
    pallas_call x1, Pallas kernels, shards(): pl.pallas_call(functools.partial(kernel, sizes), out_shape=(held, held),...  18.6 us
    pallas_call x1, Pallas kernels, shards(): pl.pallas_call(deliver, out_shape=(out, out), in_specs=[pl.BlockSpec(memo...  0.66 us

profile of v6, /device:TPU:0, one launch (start us, length us, event | category | flops | bytes accessed | tf_op | source)
XLA Modules:
  0.0 19.9 jit_solution(9905306516803648088)
XLA Ops:
  0.6 18.6 %shard_map.41 = (f32[1,1,1,128,128]{4,3,2,1,0:T(8,128)S(1)}, f32[1,1,1,128,128]{4,3,2,1,0:T(8,128)S(1)}) custom-call(f32[1,1,1,128,128]{4,3,2,1,0:T(8,128)} %b_hbm.1, f32[1,1,1,9,2,32,32,128]{7,6,5,4,3,2,1,0:T(8,128)} %l_hbm.1), custom_call_target="tpu_custom_call" | custom-call | tf_op jit(solution)/shard_map/pallas_call | solution.py:463
  19.2 0.7 %shard_map.42 = (f32[1,1,1,128,128]{4,3,2,1,0:T(8,128)}, f32[1,1,1,128,128]{4,3,2,1,0:T(8,128)}) custom-call(f32[1,1,1,128,128]{4,3,2,1,0:T(8,128)S(1)} %get-tuple-element.4.a_ref, f32[1,1,1,128,128]{4,3,2,1,0:T(8,128)S(1)} %get-tuple-element.5.b_ref), custom_call_target="tpu_custom_call" | custom-call | tf_op jit(solution)/shard_map/pallas_call | solution.py:495

commit v7 on v6

--- a/solution.py
+++ b/solution.py
@@ -122,7 +122,7 @@
     barrier = pltpu.get_barrier_semaphore()
     tell(barrier, line_t + line_z + line_x)
 
-    for number, k, count in ((0, 0, 1), (0, 3, 2), (1, 7, 2), (1, 5, 2), (2, 1, 2)):
+    for number, k, count in ((0, 7, 2), (1, 5, 2), (1, 0, 1), (2, 3, 2), (3, 1, 2)):
         part = pl.ds(k, count)
         pltpu.make_async_copy(l_hbm.at[0, 0, 0, part], links.at[part], l_sem.at[number]).start(priority=1)
 
@@ -294,24 +294,35 @@
             out.append([both[g] - (rr[g] + ii[g]) for g in range(groups)])
         return out
 
-    local = ((0, None), (3, 0), (4, 1), (7, 3), (8, 4), (5, 2))
+    local = ((7, 3), (8, 4), (5, 2), (0, None), (3, 0), (4, 1))
+
+    def near_of(n, terms):
+        return [(link, kv.at[n] if near is None else turned.at[near]) for link, near in terms]
+
+    def local_first():
+        wait_links(0, 2)
+        products(near_of(0, local[:2]), True)
+        pack_edges()
+        wait_links(1, 3)
+        split_z()
+        products(near_of(0, local[2:4]), False)
 
     def apply(n):
-        shift(n)
-        terms = [(link, kv.at[n] if near is None else turned.at[near]) for link, near in local]
         if n == 0:
-            wait_links(0, 3)
-            products(terms[:3], True)
-            wait_links(1, 4)
-            products(terms[3:5], False)
-            pack_edges()
-            split_z()
-            products(terms[5:], False)
+
+            @pl.when(it != 0)
+            def _():
+                shift(0)
+                local_first()
+
+            wait_links(2, 2)
+            products(near_of(0, local[4:]), False)
             pl.semaphore_wait(seen_z, len(line_z))
             tell(seen_x, line_x)
-            wait_links(2, 2)
+            wait_links(3, 2)
         else:
-            products(terms, True)
+            shift(1)
+            products(near_of(1, local), True)
             early()
         receive(n, 1, xbuf.at[n, pl.ds(0, ways)])
         if nx > 2:
@@ -388,6 +399,12 @@
 
     b_copy.wait()
     kv[0] = field[0].T
+
+    @pl.when(it == 0)
+    def _():
+        shift(0)
+        local_first()
+
     pl.semaphore_wait(barrier, len(line_t) + len(line_z) + len(line_x))
     halo(0)
     tell(seen_z, line_z)
@@ -481,7 +498,7 @@
             pltpu.VMEM((4, DOF, 8, S), f32),
             pltpu.VMEM((nx * nz * nt, 1, 128), f32),
             pltpu.SemaphoreType.DMA,
-            pltpu.SemaphoreType.DMA((3,)),
+            pltpu.SemaphoreType.DMA((4,)),
             pltpu.SemaphoreType.DMA((2,)),
             pltpu.SemaphoreType.DMA((2, 4)),
             pltpu.SemaphoreType.DMA,

time: 20 us -> 19.8 us (0.990)
    pallas_call x1, Pallas kernels: 18.6 us -> 18.3 us  [shards(): pl.pallas_call(functools.partial(kernel, sizes), out_shape=(held, held),...]
where the time goes in v7:
time: 19.8 us; the launch traced here: 19.6 us
  Pallas kernels  19 us (96%)
  between operations  0.64 us (3%)
    pallas_call x1, Pallas kernels, shards(): pl.pallas_call(functools.partial(kernel, sizes), out_shape=(held, held),...  18.3 us
    pallas_call x1, Pallas kernels, shards(): pl.pallas_call(deliver, out_shape=(out, out), in_specs=[pl.BlockSpec(memo...  0.66 us

profile of v7, /device:TPU:0, one launch (start us, length us, event | category | flops | bytes accessed | tf_op | source)
XLA Modules:
  0.0 19.6 jit_solution(54018043267930965)
XLA Ops:
  0.6 18.3 %shard_map.41 = (f32[1,1,1,128,128]{4,3,2,1,0:T(8,128)S(1)}, f32[1,1,1,128,128]{4,3,2,1,0:T(8,128)S(1)}) custom-call(f32[1,1,1,128,128]{4,3,2,1,0:T(8,128)} %b_hbm.1, f32[1,1,1,9,2,32,32,128]{7,6,5,4,3,2,1,0:T(8,128)} %l_hbm.1), custom_call_target="tpu_custom_call" | custom-call | tf_op jit(solution)/shard_map/pallas_call | solution.py:480
  18.9 0.7 %shard_map.42 = (f32[1,1,1,128,128]{4,3,2,1,0:T(8,128)}, f32[1,1,1,128,128]{4,3,2,1,0:T(8,128)}) custom-call(f32[1,1,1,128,128]{4,3,2,1,0:T(8,128)S(1)} %get-tuple-element.4.a_ref, f32[1,1,1,128,128]{4,3,2,1,0:T(8,128)S(1)} %get-tuple-element.5.b_ref), custom_call_target="tpu_custom_call" | custom-call | tf_op jit(solution)/shard_map/pallas_call | solution.py:512

commit v8 on v7

--- a/solution.py
+++ b/solution.py
@@ -467,9 +467,12 @@
     remote(others, others, sent.at[1], got_sum, (ix, iz, it)).wait_send()
 
 
-def deliver(a_ref, b_ref, sol_ref, res_ref):
-    sol_ref[...] = a_ref[...]
-    res_ref[...] = b_ref[...]
+def deliver(a_ref, b_ref, sol_ref, res_ref, sems):
+    copies = [pltpu.make_async_copy(a_ref, sol_ref, sems.at[0]), pltpu.make_async_copy(b_ref, res_ref, sems.at[1])]
+    for copy in copies:
+        copy.start()
+    for copy in copies:
+        copy.wait()
 
 
 def shards(sizes, right_side, link_blocks):
@@ -513,7 +516,8 @@
         deliver,
         out_shape=(out, out),
         in_specs=[pl.BlockSpec(memory_space=pltpu.VMEM)] * 2,
-        out_specs=(pl.BlockSpec(memory_space=pltpu.VMEM),) * 2,
+        out_specs=(pl.BlockSpec(memory_space=pl.ANY),) * 2,
+        scratch_shapes=[pltpu.SemaphoreType.DMA((2,))],
     )(*[pltpu.with_memory_space_constraint(x, pltpu.VMEM) for x in results])
 
 

time: 19.8 us -> 19.8 us (level)
  no operation moved by 1% of the time
where the time goes in v8:
time: 19.8 us; the launch traced here: 19.6 us
  Pallas kernels  19 us (96%)
  between operations  0.64 us (3%)
    pallas_call x1, Pallas kernels, shards(): pl.pallas_call(functools.partial(kernel, sizes), out_shape=(held, held),...  18.3 us
    pallas_call x1, Pallas kernels, shards(): pl.pallas_call(deliver, out_shape=(out, out), in_specs=[pl.BlockSpec(memo...  0.67 us

profile of v8, /device:TPU:0, one launch (start us, length us, event | category | flops | bytes accessed | tf_op | source)
XLA Modules:
  0.0 19.6 jit_solution(14451652775202566063)
XLA Ops:
  0.6 18.3 %shard_map.41 = (f32[1,1,1,128,128]{4,3,2,1,0:T(8,128)S(1)}, f32[1,1,1,128,128]{4,3,2,1,0:T(8,128)S(1)}) custom-call(f32[1,1,1,128,128]{4,3,2,1,0:T(8,128)} %b_hbm.1, f32[1,1,1,9,2,32,32,128]{7,6,5,4,3,2,1,0:T(8,128)} %l_hbm.1), custom_call_target="tpu_custom_call" | custom-call | tf_op jit(solution)/shard_map/pallas_call | solution.py:483
  18.9 0.7 %shard_map.42 = (f32[1,1,1,128,128]{4,3,2,1,0:T(8,128)}, f32[1,1,1,128,128]{4,3,2,1,0:T(8,128)}) custom-call(f32[1,1,1,128,128]{4,3,2,1,0:T(8,128)S(1)} %get-tuple-element.4.a_ref, f32[1,1,1,128,128]{4,3,2,1,0:T(8,128)S(1)} %get-tuple-element.5.b_ref), custom_call_target="tpu_custom_call" | custom-call | tf_op jit(solution)/shard_map/pallas_call | solution.py:515
